TPU v7x, 32 devices: a whole 2x2x4 slice. The times are simulated.
32 devices in a mesh: data: 32 (over z, y, x, core).
Axes of the slice: x: 2, y: 2, z: 4, core: 2. Of those that a mesh axis runs over, the one named last changes fastest.
Arguments:
- act_in: bfloat16 [131072, 960], P('data')
- grad_out: bfloat16 [131072, 960], P('data')
- w_up1: bfloat16 [960, 2560], replicated
- w_down1: bfloat16 [2560, 960], replicated
- w_up2: bfloat16 [960, 2560], replicated
- w_down2: bfloat16 [2560, 960], replicated
- master_up1: float32 [960, 2560], P('data')
- master_down1: float32 [2560, 960], P('data')
- master_up2: float32 [960, 2560], P('data')
- master_down2: float32 [2560, 960], P('data')
- mom_up1: float32 [960, 2560], P('data')
- mom_down1: float32 [2560, 960], P('data')
- mom_up2: float32 [960, 2560], P('data')
- mom_down2: float32 [2560, 960], P('data')
- vel_up1: float32 [960, 2560], P('data')
- vel_down1: float32 [2560, 960], P('data')
- vel_up2: float32 [960, 2560], P('data')
- vel_down2: float32 [2560, 960], P('data')
- learn_rate: float32 [], replicated
- clip_norm: float32 [], replicated
Outputs:
- output 1: bfloat16 [960, 2560], replicated
- output 2: bfloat16 [2560, 960], replicated
- output 3: bfloat16 [960, 2560], replicated
- output 4: bfloat16 [2560, 960], replicated
- output 5: float32 [960, 2560], P('data')
- output 6: float32 [2560, 960], P('data')
- output 7: float32 [960, 2560], P('data')
- output 8: float32 [2560, 960], P('data')
- output 9: float32 [960, 2560], P('data')
- output 10: float32 [2560, 960], P('data')
- output 11: float32 [960, 2560], P('data')
- output 12: float32 [2560, 960], P('data')
- output 13: float32 [960, 2560], P('data')
- output 14: float32 [2560, 960], P('data')
- output 15: float32 [960, 2560], P('data')
- output 16: float32 [2560, 960], P('data')
- output 17: float32 [], replicated
All inputs are finite; a program needn't handle non-finite values.
Results may differ from a plain program's by a relative error of at most 0.0117184.
Values are sent between devices in bfloat16 or wider.
A program may use at most 1 GiB of HBM per device.

v0:
```python
import math
import jax
import jax.numpy as jnp
from jax import lax
from jax.sharding import PartitionSpec as P, NamedSharding

STEP = 20
BETA_ONE = 0.9
BETA_TWO = 0.95
EPSILON = 1e-8
NORM_EPS = 1e-6
CORR_ONE = 1.0 - BETA_ONE ** STEP
CORR_TWO = 1.0 - BETA_TWO ** STEP
ROOT_HALF = math.sqrt(0.5)
INV_ROOT_TAU = 1.0 / math.sqrt(2.0 * math.pi)


def mat_nt(left, right):
    return lax.dot_general(left, right, (((1,), (1,)), ((), ())), preferred_element_type=jnp.float32)


def mat_tn(left, right):
    return lax.dot_general(left, right, (((0,), (0,)), ((), ())), preferred_element_type=jnp.float32)


def gelu_pair(pre):
    normal_cdf = 0.5 * (1.0 + lax.erf(pre * ROOT_HALF))
    density = jnp.exp(-0.5 * pre * pre) * INV_ROOT_TAU
    return pre * normal_cdf, normal_cdf + pre * density


def fwd_bwd(rows_in, rows_grad, w_up1, w_down1, w_up2, w_down2):
    pre_up1 = jnp.dot(rows_in, w_up1, preferred_element_type=jnp.float32)
    gel_up1, der_up1 = gelu_pair(pre_up1)
    act_up1 = gel_up1.astype(jnp.bfloat16)
    mid_act = jnp.dot(act_up1, w_down1, preferred_element_type=jnp.float32).astype(jnp.bfloat16)
    pre_up2 = jnp.dot(mid_act, w_up2, preferred_element_type=jnp.float32)
    gel_up2, der_up2 = gelu_pair(pre_up2)
    act_up2 = gel_up2.astype(jnp.bfloat16)
    grad_act2 = mat_nt(rows_grad, w_down2).astype(jnp.bfloat16)
    grad_pre2 = (grad_act2.astype(jnp.float32) * der_up2).astype(jnp.bfloat16)
    grad_mid = mat_nt(grad_pre2, w_up2).astype(jnp.bfloat16)
    grad_act1 = mat_nt(grad_mid, w_down1).astype(jnp.bfloat16)
    grad_pre1 = (grad_act1.astype(jnp.float32) * der_up1).astype(jnp.bfloat16)
    return ((act_up2, rows_grad), (mid_act, grad_pre2), (act_up1, grad_mid), (rows_in, grad_pre1))


def adam_step(grad_rows, master_old, mom_old, vel_old, clip_scale, learn_rate):
    scaled = clip_scale * grad_rows
    mom_new = BETA_ONE * mom_old + (1.0 - BETA_ONE) * scaled
    vel_new = BETA_TWO * vel_old + (1.0 - BETA_TWO) * scaled * scaled
    master_new = master_old - learn_rate * (mom_new / CORR_ONE) / (jnp.sqrt(vel_new / CORR_TWO) + EPSILON)
    return master_new.astype(jnp.bfloat16), master_new, mom_new, vel_new


def solution(mesh):
    groups = mesh.shape["data"]
    rows_spec = P("data", None)
    full_spec = P(None, None)
    scalar_spec = P()

    def shard_body(act_in, grad_out, w_up1, w_down1, w_up2, w_down2, master_up1, master_down1, master_up2, master_down2, mom_up1, mom_down1, mom_up2, mom_down2, vel_up1, vel_down1, vel_up2, vel_down2, learn_rate, clip_norm):
        grad_pairs = fwd_bwd(act_in, grad_out, w_up1, w_down1, w_up2, w_down2)
        shards = []
        for layer_in, layer_delta in grad_pairs:
            local_grad = mat_tn(layer_in, layer_delta)
            shards.append(lax.psum_scatter(local_grad, "data", scatter_dimension=0, tiled=True) / groups)
        grad_list = shards[::-1]
        local_sq = sum(jnp.sum(grad_rows * grad_rows) for grad_rows in grad_list)
        grad_norm = jnp.sqrt(lax.psum(local_sq, "data"))
        clip_scale = jnp.minimum(1.0, clip_norm / (grad_norm + NORM_EPS))
        master_list = (master_up1, master_down1, master_up2, master_down2)
        mom_list = (mom_up1, mom_down1, mom_up2, mom_down2)
        vel_list = (vel_up1, vel_down1, vel_up2, vel_down2)
        layer_states = [adam_step(grad_list[layer_idx], master_list[layer_idx], mom_list[layer_idx], vel_list[layer_idx], clip_scale, learn_rate) for layer_idx in range(4)]
        new_weights = [lax.all_gather(layer_state[0], "data", axis=0, tiled=True) for layer_state in layer_states]
        results = new_weights
        for field_idx in range(1, 4):
            results = results + [layer_state[field_idx] for layer_state in layer_states]
        return tuple(results + [grad_norm])

    in_specs = (rows_spec, rows_spec) + (full_spec,) * 4 + (rows_spec,) * 12 + (scalar_spec, scalar_spec)
    out_specs = (full_spec,) * 4 + (rows_spec,) * 12 + (scalar_spec,)
    return jax.shard_map(shard_body, mesh=mesh, in_specs=in_specs, out_specs=out_specs, check_vma=False)
```

profile of v0, /device:TPU:0, one launch (start us, length us, event | category | flops | bytes accessed | tf_op | source)
XLA Modules:
  0.0 1029.9 jit_solution(10433870690141830325)
XLA Ops:
  7.3 34.0 %multiply_convert_fusion.1 = (bf16[4096,2560]{1,0:T(8,128)(2,1)}, f32[4096,2560]{1,0:T(8,128)}) fusion(bf16[4096,960]{0,1:T(8,128)(2,1)} %param.20, bf16[960,2560]{1,0:T(8,128)(2,1)} %param.22), kind=kOutput, calls=%fused_computation.16 | convolution fusion | flops 20185088000 | bytes 75694080 | tf_op jit(solution)/shard_map/dot_general | solution.py:33
  41.3 25.1 %convolution_convert_fusion.3 = bf16[4096,960]{0,1:T(8,128)(2,1)} fusion(bf16[4096,2560]{1,0:T(8,128)(2,1)} %get-tuple-element.88, bf16[2560,960]{0,1:T(8,128)(2,1)S(1)} %copy-done.3), kind=kOutput, calls=%fused_computation.22 | convolution fusion | flops 20136591360 | bytes 33751040 | tf_op jit(solution)/shard_map/dot_general | solution.py:36
  66.4 28.3 %fusion.28 = f32[4096,2560]{1,0:T(8,128)} fusion(bf16[4096,960]{0,1:T(8,128)(2,1)} %convolution_convert_fusion.3, bf16[960,2560]{1,0:T(8,128)(2,1)S(1)} %bitcast.41), kind=kOutput, calls=%fused_computation.50 | convolution fusion | flops 20132659200 | bytes 54722560 | tf_op jit(solution)/shard_map/dot_general | solution.py:37
  94.8 42.3 %fusion.7 = bf16[4096,2560]{1,0:T(8,128)(2,1)} fusion(f32[4096,2560]{1,0:T(8,128)} %fusion.28, bf16[4096,960]{0,1:T(8,128)(2,1)S(1)} %bitcast.35, bf16[2560,960]{0,1:T(8,128)(2,1)S(1)} %bitcast.39), kind=kOutput, calls=%fused_computation.7 | convolution fusion | flops 20258488320 | bytes 75694080 | tf_op jit(solution)/shard_map/dot_general | solution.py:19
  137.0 23.6 %convolution_convert_fusion.2 = bf16[4096,960]{0,1:T(8,128)(2,1)S(1)} fusion(bf16[4096,2560]{1,0:T(8,128)(2,1)} %fusion.7, bf16[960,2560]{1,0:T(8,128)(2,1)S(1)} %bitcast.41), kind=kOutput, calls=%fused_computation.21 | convolution fusion | flops 20136591360 | bytes 33751040 | tf_op jit(solution)/shard_map/dot_general | solution.py:19
  160.6 3.2 copy-done.4
  163.8 26.5 %fusion.29 = f32[2560,960]{1,0:T(8,128)} fusion(bf16[4096,2560]{1,0:T(8,128)(2,1)} %get-tuple-element.88, bf16[4096,960]{0,1:T(8,128)(2,1)S(1)} %convolution_convert_fusion.2), kind=kOutput, calls=%fused_computation.51 | convolution fusion | flops 20132659200 | bytes 38666240 | tf_op jit(solution)/shard_map/dot_general | solution.py:23
  190.4 30.6 %fusion.14 = f32[2560,960]{1,0:T(8,128)} fusion(bf16[4096,960]{0,1:T(8,128)(2,1)} %param.21, f32[4096,2560]{1,0:T(8,128)} %fusion.28), kind=kOutput, calls=%fused_computation.20 | convolution fusion | flops 20185088000 | bytes 59637760 | tf_op jit(solution)/shard_map/dot_general | solution.py:23
  221.0 27.1 %fusion.30 = f32[960,2560]{1,0:T(8,128)} fusion(bf16[4096,960]{0,1:T(8,128)(2,1)} %convolution_convert_fusion.3, bf16[4096,2560]{1,0:T(8,128)(2,1)} %fusion.7), kind=kOutput, calls=%fused_computation.52 | convolution fusion | flops 20132659200 | bytes 38666240 | tf_op jit(solution)/shard_map/dot_general | solution.py:23
  248.2 43.1 %fusion.13.clone.4 = bf16[4096,2560]{1,0:T(8,128)(2,1)} fusion(f32[4096,2560]{1,0:T(8,128)} %get-tuple-element.89, bf16[4096,960]{0,1:T(8,128)(2,1)} %copy-done.4, bf16[2560,960]{0,1:T(8,128)(2,1)} %param.23), kind=kOutput, calls=%fused_computation.13.clone.clone.clone.1 | convolution fusion | flops 20258488320 | bytes 75694080 | tf_op jit(solution)/shard_map/dot_general | solution.py:19
  291.2 24.7 %convolution_bitcast_fusion = f32[960,2560]{1,0:T(8,128)} fusion(bf16[4096,960]{0,1:T(8,128)(2,1)S(1)} %bitcast.37, bf16[4096,2560]{1,0:T(8,128)(2,1)} %fusion.13.clone.4), kind=kOutput, calls=%fused_computation.23 | convolution fusion | flops 20132659200 | bytes 38666240 | tf_op jit(solution)/shard_map/dot_general | solution.py:23
  315.9 340.4 %fusion.21 = (f32[32,2560]{1,0:T(8,128)S(1)}, f32[32,2560]{1,0:T(8,128)S(1)}) fusion(f32[960,2560]{1,0:T(8,128)} %convolution_bitcast_fusion, f32[960,2560]{1,0:T(8,128)} %fusion.30), kind=kCustom, calls=%all-reduce-scatter.2 | all-reduce-scatter fusion | flops 5242881 | bytes 20316160
  656.4 9.7 collective-permute-start
  666.0 5.1 collective-permute-start.2
  672.6 8.7 collective-permute-start.3
  685.0 3.6 collective-permute-done.3
  688.6 3.3 concatenate.1
  693.3 1.7 multiply_reduce_fusion.2
  696.9 1.7 multiply_reduce_fusion
  699.3 42.7 %psum.7 = f32[]{:T(128)} all-reduce(f32[]{:T(128)S(6)} %add.76), channel_id=1, replica_groups=mesh['data'=32] {'data'}, use_global_device_ids=true, to_apply=%region_8.0 | all-reduce | flops 1 | bytes 8 | tf_op jit(solution)/shard_map/psum | solution.py:70
  742.7 2.2 fusion.22
  745.0 2.3 convert_bitcast_fusion
  747.4 2.4 fusion.25
  749.9 2.3 convert_bitcast_fusion.1
  752.2 59.2 %all-gather.9.cloned.1.call-done = bf16[2560,960]{1,0:T(8,128)(2,1)} async-done(((bf16[80,960]{1,0:T(8,128)(2,1)}), bf16[2560,960]{1,0:T(8,128)(2,1)}) %all-gather.9.cloned.1.call-update) | async-done | bytes 4915216 | tf_op jit(solution)/shard_map/all_gather | solution.py:76
  811.4 7.9 copy.42
  819.3 59.7 %all-gather.13.cloned.1.call-done = bf16[32,30,2560]{2,1,0:T(8,128)(2,1)} async-done(((bf16[1,30,2560]{2,1,0:T(8,128)(2,1)}), bf16[32,30,2560]{2,1,0:T(8,128)(2,1)}) %all-gather.13.cloned.1.call-update) | async-done | bytes 4915216 | tf_op jit(solution)/shard_map/all_gather | solution.py:76
  878.9 7.5 reshape.37
  886.4 60.1 %all-gather.7.cloned.1.call-done = bf16[2560,960]{1,0:T(8,128)(2,1)} async-done(((bf16[80,960]{1,0:T(8,128)(2,1)}), bf16[2560,960]{1,0:T(8,128)(2,1)}) %all-gather.7.cloned.1.call-update) | async-done | bytes 4915216 | tf_op jit(solution)/shard_map/all_gather | solution.py:76
  946.5 7.9 copy.41
  954.3 59.7 %all-gather.11.cloned.1.call-done = bf16[32,30,2560]{2,1,0:T(8,128)(2,1)} async-done(((bf16[1,30,2560]{2,1,0:T(8,128)(2,1)}), bf16[32,30,2560]{2,1,0:T(8,128)(2,1)}) %all-gather.11.cloned.1.call-update) | async-done | bytes 4915216 | tf_op jit(solution)/shard_map/all_gather | solution.py:76
  1014.0 7.5 reshape.35
  (52 shorter events, 5.6 us)
Async XLA Ops:
  7.2 686.1 %reduce-scatter.7.cloned.1.call-start = ((), (), s32[]{:S(2)}) async-start(), calls=%async_computation.2 | async-start | bytes 10813440 | tf_op jit(solution)/shard_map/reduce_scatter | solution.py:67
  7.2 34.1 %copy-start.3 = (bf16[2560,960]{0,1:T(8,128)(2,1)S(1)}, bf16[2560,960]{0,1:T(8,128)(2,1)}, u32[]{:S(2)}) copy-start(bf16[2560,960]{0,1:T(8,128)(2,1)} %param.23) | copy-start | bytes 14745604
  7.2 59.1 %slice-start.6 = ((s8[4915200]{0:T(1024)(128)(4,1)}), s8[4194304]{0:T(1024)(128)(4,1)S(1)}, s32[]{:S(2)}) async-start(s8[4915200]{0:T(1024)(128)(4,1)} %bitcast.40), calls=%async_computation.14 | async-start | bytes 8388608
  41.3 25.1 %slice-start.7 = ((s8[4915200]{0:T(1024)(128)(4,1)}), s8[720896]{0:T(1024)(128)(4,1)S(1)}, s32[]{:S(2)}) async-start(s8[4915200]{0:T(1024)(128)(4,1)} %bitcast.40), calls=%async_computation.15 | async-start | bytes 1441792
  41.3 53.4 %slice-start = ((s8[7864320]{0:T(1024)(128)(4,1)}), s8[4194304]{0:T(1024)(128)(4,1)S(1)}, s32[]{:S(2)}) async-start(s8[7864320]{0:T(1024)(128)(4,1)} %bitcast.34), calls=%async_computation.8 | async-start | bytes 8388608
  41.3 53.4 %slice-start.4 = ((s8[4915200]{0:T(1024)(128)(4,1)}), s8[4194304]{0:T(1024)(128)(4,1)S(1)}, s32[]{:S(2)}) async-start(s8[4915200]{0:T(1024)(128)(4,1)} %bitcast.38), calls=%async_computation.12 | async-start | bytes 8388608
  66.4 28.4 %slice-start.1 = ((s8[7864320]{0:T(1024)(128)(4,1)}), s8[3670016]{0:T(1024)(128)(4,1)S(1)}, s32[]{:S(2)}) async-start(s8[7864320]{0:T(1024)(128)(4,1)} %bitcast.34), calls=%async_computation.9 | async-start | bytes 7340032
  66.4 28.3 %slice-start.5 = ((s8[4915200]{0:T(1024)(128)(4,1)}), s8[720896]{0:T(1024)(128)(4,1)S(1)}, s32[]{:S(2)}) async-start(s8[4915200]{0:T(1024)(128)(4,1)} %bitcast.38), calls=%async_computation.13 | async-start | bytes 1441792
  160.6 3.2 copy-start.4
  190.3 506.6 %reduce-scatter.9.cloned.1.call-start = ((), (), s32[]{:S(2)}) async-start(), calls=%async_computation.3 | async-start | bytes 10813440 | tf_op jit(solution)/shard_map/reduce_scatter | solution.py:67
  221.0 590.4 %all-gather.9.cloned.1.call-start = ((), (), s32[]{:S(2)}) async-start(), calls=%async_computation.5 | async-start | bytes 5406720 | tf_op jit(solution)/shard_map/all_gather | solution.py:76
  221.0 70.2 %slice-start.2 = ((s8[7864320]{0:T(1024)(128)(4,1)}), s8[4194304]{0:T(1024)(128)(4,1)S(1)}, s32[]{:S(2)}) async-start(s8[7864320]{0:T(1024)(128)(4,1)} %bitcast.36), calls=%async_computation.10 | async-start | bytes 8388608
  248.2 43.1 %slice-start.3 = ((s8[7864320]{0:T(1024)(128)(4,1)}), s8[3670016]{0:T(1024)(128)(4,1)S(1)}, s32[]{:S(2)}) async-start(s8[7864320]{0:T(1024)(128)(4,1)} %bitcast.36), calls=%async_computation.11 | async-start | bytes 7340032
  315.9 426.8 %copy-start = (f32[80,960]{1,0:T(8,128)S(1)}, f32[80,960]{1,0:T(8,128)}, u32[]{:S(2)}) copy-start(f32[80,960]{1,0:T(8,128)} %param.29) | copy-start | bytes 921604
  315.9 426.8 %copy-start.1 = (f32[80,960]{1,0:T(8,128)S(1)}, f32[80,960]{1,0:T(8,128)}, u32[]{:S(2)}) copy-start(f32[80,960]{1,0:T(8,128)} %param.33) | copy-start | bytes 921604
  656.4 27.0 %collective-permute-start = (f32[32,2560]{1,0:T(8,128)S(1)}, f32[32,2560]{1,0:T(8,128)S(1)}, u32[]{:S(2)}, u32[]{:S(2)}) collective-permute-start(f32[32,2560]{1,0:T(8,128)S(1)} %get-tuple-element.70), channel_id=1, source_target_pairs={{0,1},{1,2},{2,3},{3,4},{4,5},{5,6},{6,7},{7,8},{8,9},{9,10},{10,1... | collective-permute-start | bytes 983048
  666.0 22.6 %collective-permute-start.2 = (f32[32,2560]{1,0:T(8,128)S(1)}, f32[32,2560]{1,0:T(8,128)}, u32[]{:S(2)}, u32[]{:S(2)}) collective-permute-start(f32[32,2560]{1,0:T(8,128)S(1)} %get-tuple-element.71), channel_id=1, source_target_pairs={{0,1},{1,2},{2,3},{3,4},{4,5},{5,6},{6,7},{7,8},{8,9},{9,10},{10,1... | collective-permute-start | bytes 983048
  671.2 11.4 %collective-permute-start.1 = (f32[30,2560]{1,0:T(8,128)S(1)}, f32[30,2560]{1,0:T(8,128)S(1)}, u32[]{:S(2)}, u32[]{:S(2)}) collective-permute-start(f32[30,2560]{1,0:T(8,128)S(1)} %slice), channel_id=1, source_target_pairs={{0,2},{1,3},{2,4},{3,5},{4,6},{5,7},{6,8},{7,9},{8,10},{9,11},{10,... | collective-permute-start | bytes 921608
  672.6 16.1 %collective-permute-start.3 = (f32[30,2560]{1,0:T(8,128)S(1)}, f32[30,2560]{1,0:T(8,128)}, u32[]{:S(2)}, u32[]{:S(2)}) collective-permute-start(f32[30,2560]{1,0:T(8,128)S(1)} %slice.1), channel_id=1, source_target_pairs={{0,2},{1,3},{2,4},{3,5},{4,6},{5,7},{6,8},{7,9},{8,10},{9,11},{10,... | collective-permute-start | bytes 921608
  682.6 0.7 copy-start.2
  744.9 134.0 %all-gather.13.cloned.1.call-start = ((), (), s32[]{:S(2)}) async-start(), calls=%async_computation.7 | async-start | bytes 5406720 | tf_op jit(solution)/shard_map/all_gather | solution.py:76
  747.3 199.1 %all-gather.7.cloned.1.call-start = ((), (), s32[]{:S(2)}) async-start(), calls=%async_computation.4 | async-start | bytes 5406720 | tf_op jit(solution)/shard_map/all_gather | solution.py:76
  749.8 264.2 %all-gather.11.cloned.1.call-start = ((), (), s32[]{:S(2)}) async-start(), calls=%async_computation.6 | async-start | bytes 5406720 | tf_op jit(solution)/shard_map/all_gather | solution.py:76
Sparse Core Ops, SparseCore 0:
  190.4 168.6 reduce-scatter.6
  361.5 231.1 reduce-scatter.8
  745.1 66.2 all-gather.8
  814.7 64.2 all-gather.12
  882.2 64.2 all-gather.6
  949.8 64.2 all-gather.10
where the time goes:
time: 1040 us; the launch traced here: 1030 us
  blocking collectives  383 us (37%)
  matrix products  305 us (29%)
  waiting for transfers between devices  242 us (23%)
  local copies, waits for them, and re-layouts  39.6 us (4%)
  starting transfers between devices  25.1 us (2%)
  between operations  20.6 us (2%)
  other arithmetic  13.9 us (1%)
    unnamed x1, blocking collectives  340 us
    all_gather x4, waiting for transfers between devices, shard_body(): lax.all_gather(layer_state[0], 'data', axis=0, tiled=True)  239 us
    dot_general x4, matrix products, mat_tn(): lax.dot_general(left, right, (((0,), (0,)), ((), ())), preferred_element_...  109 us
    dot_general x3, matrix products, mat_nt(): lax.dot_general(left, right, (((1,), (1,)), ((), ())), preferred_element_...  109 us
    psum x1, blocking collectives, shard_body(): grad_norm = jnp.sqrt(lax.psum(local_sq, 'data'))  42.7 us
    unnamed x34, local copies, waits for them, and re-layouts  39.6 us
    dot_general x1, matrix products, fwd_bwd(): pre_up1 = jnp.dot(rows_in, w_up1, preferred_element_type=jnp.float32)  34 us
    dot_general x1, matrix products, fwd_bwd(): pre_up2 = jnp.dot(mid_act, w_up2, preferred_element_type=jnp.float32)  28.3 us
  transfers between devices with their start and end apart: 10, of which 5 were waited for; matrix products, arithmetic and copies ran while one was open for 49% of the time, Pallas kernels for 0%

commit v1 on v0

v1 whole, which is shorter than its diff:
```python
import functools
import math
import jax
import jax.numpy as jnp
from jax import lax
from jax.experimental import pallas as pl
from jax.experimental.pallas import tpu as pltpu
from jax.sharding import PartitionSpec as P

STEP = 20
BETA_ONE = 0.9
BETA_TWO = 0.95
EPSILON = 1e-8
NORM_EPS = 1e-6
CORR_ONE = 1.0 - BETA_ONE ** STEP
CORR_TWO = 1.0 - BETA_TWO ** STEP
ROOT_HALF = math.sqrt(0.5)
INV_ROOT_TAU = 1.0 / math.sqrt(2.0 * math.pi)
D, FF, DEVS = 960, 2560, 32
UP, DOWN = D // DEVS, FF // DEVS

ORDERS = ((1, 2, 4, 8, 16), (1, 4, 2, 8, 16), (1, 8, 4, 2, 16))
SIZES = (16, 8, 4, 2, 1)
BASES = (0, 16, 24, 28, 30)
KINDS = ("down", "up", "down", "up")
CHUNKS = 10
PARTS = 5


def mat_nt(left, right):
    return lax.dot_general(left, right, (((1,), (1,)), ((), ())), preferred_element_type=jnp.float32)


def mat_tn(left, right):
    return lax.dot_general(left, right, (((0,), (0,)), ((), ())), preferred_element_type=jnp.float32)


def gelu_pair(pre):
    normal_cdf = 0.5 * (1.0 + lax.erf(pre * ROOT_HALF))
    density = jnp.exp(-0.5 * pre * pre) * INV_ROOT_TAU
    return pre * normal_cdf, normal_cdf + pre * density


def fwd_bwd(rows_in, rows_grad, w_up1, w_down1, w_up2, w_down2):
    pre_up1 = jnp.dot(rows_in, w_up1, preferred_element_type=jnp.float32)
    gel_up1, der_up1 = gelu_pair(pre_up1)
    act_up1 = gel_up1.astype(jnp.bfloat16)
    mid_act = jnp.dot(act_up1, w_down1, preferred_element_type=jnp.float32).astype(jnp.bfloat16)
    pre_up2 = jnp.dot(mid_act, w_up2, preferred_element_type=jnp.float32)
    gel_up2, der_up2 = gelu_pair(pre_up2)
    act_up2 = gel_up2.astype(jnp.bfloat16)
    grad_act2 = mat_nt(rows_grad, w_down2).astype(jnp.bfloat16)
    grad_pre2 = (grad_act2.astype(jnp.float32) * der_up2).astype(jnp.bfloat16)
    grad_mid = mat_nt(grad_pre2, w_up2).astype(jnp.bfloat16)
    grad_act1 = mat_nt(grad_mid, w_down1).astype(jnp.bfloat16)
    grad_pre1 = (grad_act1.astype(jnp.float32) * der_up1).astype(jnp.bfloat16)
    return ((act_up2, rows_grad), (mid_act, grad_pre2), (act_up1, grad_mid), (rows_in, grad_pre1))


def position(dev, order):
    return sum(((dev // bit) % 2) * size for bit, size in zip(order, SIZES))


class Route:
    def __init__(self):
        self.me = lax.axis_index("data")
        self.bits = {bit: (self.me // bit) % 2 for bit in (1, 2, 4, 8, 16)}
        self.peers = {bit: self.me + bit * (1 - 2 * self.bits[bit]) for bit in (1, 2, 4, 8, 16)}

    def start_of(self, order, stage):
        return sum((self.bits[order[k]] * SIZES[k] for k in range(stage)), 0)


def barrier_with(peers):
    sem = pltpu.get_barrier_semaphore()
    for peer in peers:
        pl.semaphore_signal(sem, inc=1, device_id=(peer,), device_id_type=pl.DeviceIdType.MESH)
    pl.semaphore_wait(sem, len(peers))


def stream_chunk(stream, i):
    per = (4, 3, 3)[stream]
    return (i // per) * CHUNKS + stream + 3 * (i % per)


def reduce_tick(route, t, gbuf, recv, ssem, rsem, gsh):
    for stream, order in enumerate(ORDERS):
        count = (16, 12, 12)[stream]
        for stage in (5, 4, 3, 2, 1, 0):
            i = t - stage

            @pl.when((i >= 0) & (i < count))
            def _(stream=stream, order=order, stage=stage, i=i):
                c = stream_chunk(stream, i)
                slot = lax.rem(i, 2)

                def copy(k):
                    bit, n = order[k], SIZES[k]
                    away = route.start_of(order, k) + (1 - route.bits[bit]) * n
                    return pltpu.make_async_remote_copy(
                        src_ref=gbuf.at[c, pl.ds(away, n)],
                        dst_ref=recv.at[stream, slot, pl.ds(BASES[k], n)],
                        send_sem=ssem.at[stream, slot, k], recv_sem=rsem.at[stream, slot, k],
                        device_id=(route.peers[bit],), device_id_type=pl.DeviceIdType.MESH)

                if stage > 0:
                    last = stage - 1
                    copy(last).wait()
                    kept, n = route.start_of(order, stage), SIZES[last]
                    if stage < 5:
                        for b in range(n):
                            gbuf[c, kept + b] += recv[stream, slot, BASES[last] + b]
                    else:
                        gsh[c] = (gbuf[c, kept] + recv[stream, slot, BASES[last]]) * (1.0 / DEVS)
                if stage < 5:
                    copy(stage).start()


def repack_up(tile, gbuf, chunk, order):
    for dev in range(DEVS):
        pos = position(dev, order)
        for group in range(4):
            rows = min(8, UP - 8 * group)
            gbuf[chunk, pos, 0:rows, 256 * group:256 * (group + 1)] = tile[UP * dev + 8 * group:UP * dev + 8 * group + rows, :]
        gbuf[chunk, pos, 6:8, 768:1024] = jnp.zeros((2, 256), jnp.float32)


def reduce_kernel(g4, g3, g2, g1, gsh_out, norm_out, gbuf, recv, tile, gsh, sums, load_sem, tile_sem, ssem, rsem, nsend, nrecv, out_sem):
    route = Route()
    everyone = [lax.rem(route.me + k, DEVS) for k in range(1, DEVS)]
    barrier_with(everyone)

    def down_loads():
        for k, ref in ((0, g4), (2, g2)):
            for stream, order in enumerate(ORDERS):
                for j in range(stream, CHUNKS, 3):
                    for dev in range(DEVS):
                        yield pltpu.make_async_copy(ref.at[dev, pl.ds(8 * j, 8)], gbuf.at[10 * k + j, position(dev, order)], load_sem)

    for copy in down_loads():
        copy.start()

    for k, ref in ((1, g3), (3, g1)):
        def fetch(j, ref=ref):
            return pltpu.make_async_copy(ref.at[:, pl.ds(pl.multiple_of(256 * j, 256), 256)], tile.at[j % 2], tile_sem.at[j % 2])
        fetch(0).start()
        for j in range(CHUNKS):
            if j + 1 < CHUNKS:
                fetch(j + 1).start()
            fetch(j).wait()
            repack_up(tile.at[j % 2], gbuf, 10 * k + j, ORDERS[j % 3])
    for k in (0, 2):
        pltpu.make_async_copy(gbuf.at[pl.ds(10 * k, 10)], gbuf.at[pl.ds(10 * k, 10)], load_sem).wait()

    def tick(t, carry):
        reduce_tick(route, t, gbuf, recv, ssem, rsem, gsh)
        return carry
    lax.fori_loop(0, 16 + 5, tick, 0)

    out = pltpu.make_async_copy(gsh, gsh_out, out_sem)
    out.start()

    def square(c, acc):
        g = gsh[c]
        return acc + g * g
    acc = lax.fori_loop(0, 4 * CHUNKS, square, jnp.zeros((8, 1024), jnp.float32))
    part = acc[:, 0:128]
    for k in range(1, 8):
        part = part + acc[:, 128 * k:128 * (k + 1)]
    sums[route.me] = part
    def tell(peer):
        return pltpu.make_async_remote_copy(src_ref=sums.at[route.me], dst_ref=sums.at[route.me], send_sem=nsend, recv_sem=nrecv,
                                            device_id=(peer,), device_id_type=pl.DeviceIdType.MESH)
    for peer in everyone:
        tell(peer).start()
    everything = pltpu.make_async_copy(sums.at[pl.ds(0, DEVS - 1)], sums.at[pl.ds(0, DEVS - 1)], nrecv)
    everything.wait()
    pltpu.make_async_copy(sums.at[pl.ds(0, DEVS - 1)], sums.at[pl.ds(0, DEVS - 1)], nsend).wait()
    total = sums[0]
    for dev in range(1, DEVS):
        total = total + sums[dev]
    total = jnp.sum(jnp.sum(total, axis=0, keepdims=True), axis=1, keepdims=True)
    norm_out[...] = jnp.broadcast_to(jnp.sqrt(total), (8, 128))
    out.wait()


def adam(grad, mom, vel, master, scale, rate):
    scaled = scale * grad
    mom_new = BETA_ONE * mom + (1.0 - BETA_ONE) * scaled
    vel_new = BETA_TWO * vel + (1.0 - BETA_TWO) * scaled * scaled
    master_new = master - rate * (mom_new / CORR_ONE) / (jnp.sqrt(vel_new / CORR_TWO) + EPSILON)
    return master_new, mom_new, vel_new


def pieces(kind, j):
    if kind == "down":
        return [(8 * j, 8, 0, D, 0)]
    return [(8 * i, min(8, UP - 8 * i), 256 * j, 256, 256 * i) for i in range(4)]


def gather_kernel(gsh, norm, lr, clip, *refs):
    states = [refs[3 * k:3 * k + 3] for k in range(4)]
    up_out, down_out, up_buf, down_buf, fresh, ssem, rsem, out_sem = refs[12:]
    route = Route()
    peers = list(route.peers.values())
    barrier_with(peers)
    rate = lr[0]
    scale = jnp.minimum(1.0, clip[0] / (norm[0:1, 0:1] + NORM_EPS))
    fresh[...] = jnp.zeros((32, FF), jnp.float32)

    for k, kind in enumerate(KINDS):
        master, mom, vel = states[k]
        half = k // 2
        for j in range(CHUNKS):
            for row, rows, col, cols, lane in pieces(kind, j):
                at = (slice(row, row + rows), slice(col, col + cols))
                new = adam(gsh[10 * k + j, 0:rows, lane:lane + cols], mom[at], vel[at], master[at], scale, rate)[0]
                fresh[(row if kind == "up" else 8 * (j % 2)):(row if kind == "up" else 8 * (j % 2)) + rows, col:col + cols] = new
            if kind == "down" and j % 2 == 1:
                p = j // 2
                unit = 5 * k + p
                down_buf[PARTS * half + p, position(route.me, ORDERS[unit % 3])] = fresh[0:16, 0:1024].astype(jnp.bfloat16)
        if kind == "up":
            for p in range(PARTS):
                unit = 5 * k + p
                up_buf[PARTS * half + p, position(route.me, ORDERS[unit % 3])] = fresh[:, 512 * p:512 * (p + 1)].astype(jnp.bfloat16)

    def unit_ref(unit):
        k, p = unit // PARTS, unit % PARTS
        return (up_buf if KINDS[k] == "up" else down_buf).at[PARTS * (k // 2) + p]

    def out_copy(unit):
        k, p = unit // PARTS, unit % PARTS
        dst = (up_out if KINDS[k] == "up" else down_out).at[PARTS * (k // 2) + p]
        return pltpu.make_async_copy(unit_ref(unit), dst, out_sem)

    def copy(unit, stage):
        order = ORDERS[unit % 3]
        k = 4 - stage
        bit, n = order[k], SIZES[k]
        mine = route.start_of(order, k) + route.bits[bit] * n
        ref = unit_ref(unit).at[pl.ds(mine, n)]
        return pltpu.make_async_remote_copy(src_ref=ref, dst_ref=ref, send_sem=ssem.at[unit, stage], recv_sem=rsem.at[unit, stage],
                                            device_id=(route.peers[bit],), device_id_type=pl.DeviceIdType.MESH)

    for t in range(7 + 5):
        for stage in (5, 4, 3, 2, 1, 0):
            for stream in range(3):
                unit = 3 * (t - stage) + stream
                if not (t - stage >= 0 and unit < 4 * PARTS):
                    continue
                if stage > 0:
                    copy(unit, stage - 1).wait()
                if stage < 5:
                    copy(unit, stage).start()
                else:
                    out_copy(unit).start()
    for unit in range(4 * PARTS):
        out_copy(unit).wait()


def finish_kernel(up_ref, down_ref, gsh, norm, lr, clip, *refs):
    states = [refs[3 * k:3 * k + 3] for k in range(4)]
    new_up, new_down = refs[12:14]
    outs = [refs[14 + 3 * k:17 + 3 * k] for k in range(4)]
    wide, tall = refs[26:28]
    step = pl.program_id(0)

    @pl.when(step == 0)
    def _():
        rate = lr[0]
        scale = jnp.minimum(1.0, clip[0] / (norm[0:1, 0:1] + NORM_EPS))
        for k, kind in enumerate(KINDS):
            for j in range(CHUNKS):
                for row, rows, col, cols, lane in pieces(kind, j):
                    at = (slice(row, row + rows), slice(col, col + cols))
                    master, mom, vel = (r[at] for r in states[k])
                    news = adam(gsh[10 * k + j, 0:rows, lane:lane + cols], mom, vel, master, scale, rate)
                    for out, new in zip(outs[k], news):
                        out[at] = new

    half, p = step // PARTS, step % PARTS
    for stream, order in enumerate(ORDERS):
        @pl.when(lax.rem(5 * (2 * half + 1) + p, 3) == stream)
        def _(order=order):
            for dev in range(DEVS):
                wide[UP * dev:UP * (dev + 1), :] = up_ref[0, position(dev, order), 0:UP, :].astype(jnp.float32)
        @pl.when(lax.rem(5 * 2 * half + p, 3) == stream)
        def _(order=order):
            for dev in range(DEVS):
                tall[dev] = down_ref[0, position(dev, order), :, 0:D]
    new_up[0] = wide[...].astype(jnp.bfloat16)
    new_down[0] = tall[...]


def solution(mesh):
    rows_spec = P("data", None)
    full_spec = P(None, None)
    vmem = pl.BlockSpec(memory_space=pltpu.VMEM)
    smem = pl.BlockSpec(memory_space=pltpu.SMEM)
    hbm = pl.BlockSpec(memory_space=pl.ANY)
    f32, bf16 = jnp.float32, jnp.bfloat16
    dma = pltpu.SemaphoreType.DMA

    def shard_body(act_in, grad_out, w_up1, w_down1, w_up2, w_down2, master_up1, master_down1, master_up2, master_down2, mom_up1, mom_down1, mom_up2, mom_down2, vel_up1, vel_down1, vel_up2, vel_down2, learn_rate, clip_norm):
        grad_pairs = fwd_bwd(act_in, grad_out, w_up1, w_down1, w_up2, w_down2)
        local = [mat_tn(a, b) for a, b in grad_pairs]
        for k in (0, 2):
            local[k] = jnp.pad(local[k], ((0, 0), (0, 64))).reshape(DEVS, DOWN, 1024)
        gsh, norm = pl.pallas_call(
            reduce_kernel,
            out_shape=(jax.ShapeDtypeStruct((40, 8, 1024), f32), jax.ShapeDtypeStruct((8, 128), f32)),
            in_specs=[hbm] * 4, out_specs=(hbm, vmem),
            scratch_shapes=[
                pltpu.VMEM((40, 32, 8, 1024), f32), pltpu.VMEM((3, 2, 31, 8, 1024), f32), pltpu.VMEM((2, D, 256), f32),
                pltpu.VMEM((40, 8, 1024), f32), pltpu.VMEM((32, 8, 128), f32),
                dma, dma((2,)), dma((3, 2, 5)), dma((3, 2, 5)), dma, dma, dma],
            compiler_params=pltpu.CompilerParams(collective_id=0, has_side_effects=True, vmem_limit_bytes=64 * 1024 * 1024 - 65536),
            name="reduce",
        )(*local)
        states = [master_down2, mom_down2, vel_down2, master_up2, mom_up2, vel_up2, master_down1, mom_down1, vel_down1, master_up1, mom_up1, vel_up1]
        lr, clip = learn_rate.reshape(1), clip_norm.reshape(1)
        up_all, down_all = pl.pallas_call(
            gather_kernel,
            out_shape=(jax.ShapeDtypeStruct((10, 32, 32, 512), bf16), jax.ShapeDtypeStruct((10, 32, 16, 1024), bf16)),
            in_specs=[vmem, vmem, smem, smem] + [vmem] * 12, out_specs=(hbm, hbm),
            scratch_shapes=[
                pltpu.VMEM((10, 32, 32, 512), bf16), pltpu.VMEM((10, 32, 16, 1024), bf16), pltpu.VMEM((32, FF), f32),
                dma((20, 5)), dma((20, 5)), dma],
            compiler_params=pltpu.CompilerParams(collective_id=1, has_side_effects=True, vmem_limit_bytes=48 * 1024 * 1024),
            name="gather",
        )(gsh, norm, lr, clip, *states)
        whole = lambda shape: pl.BlockSpec(shape, lambda s: (0,) * len(shape))
        state_shapes = [(DOWN, D)] * 3 + [(UP, FF)] * 3 + [(DOWN, D)] * 3 + [(UP, FF)] * 3
        res = pl.pallas_call(
            finish_kernel,
            grid=(10,),
            out_shape=(jax.ShapeDtypeStruct((2, D, FF), bf16), jax.ShapeDtypeStruct((2, DEVS, DOWN, D), bf16)) + tuple(jax.ShapeDtypeStruct(s, f32) for s in state_shapes),
            in_specs=[pl.BlockSpec((1, 32, 32, 512), lambda s: (s, 0, 0, 0)), pl.BlockSpec((1, 32, 16, 1024), lambda s: (s, 0, 0, 0)),
                      whole((40, 8, 1024)), whole((8, 128)), smem, smem] + [whole(s) for s in state_shapes],
            out_specs=(pl.BlockSpec((1, D, 512), lambda s: (s // PARTS, 0, s % PARTS)), pl.BlockSpec((1, DEVS, 16, D), lambda s: (s // PARTS, 0, s % PARTS, 0))) + tuple(whole(s) for s in state_shapes),
            scratch_shapes=[pltpu.VMEM((D, 512), f32), pltpu.VMEM((DEVS, 16, D), bf16)],
            compiler_params=pltpu.CompilerParams(vmem_limit_bytes=48 * 1024 * 1024),
            name="finish",
        )(up_all, down_all, gsh, norm, lr, clip, *states)
        new_up, new_down = res[0], res[1].reshape(2, FF, D)
        st = [res[2 + 3 * k:5 + 3 * k] for k in range(4)]
        order = (3, 2, 1, 0)
        weights = (new_up[1], new_down[1], new_up[0], new_down[0])
        return weights + tuple(st[k][f] for f in range(3) for k in order) + (norm[0, 0],)

    in_specs = (rows_spec, rows_spec) + (full_spec,) * 4 + (rows_spec,) * 12 + (P(), P())
    out_specs = (full_spec,) * 4 + (rows_spec,) * 12 + (P(),)
    return jax.shard_map(shard_body, mesh=mesh, in_specs=in_specs, out_specs=out_specs, check_vma=False)
```

time: 1040 us -> 708 us (0.68)
  blocking collectives: 383 us -> 0 us
  Pallas kernels: 0 us -> 318 us
  waiting for transfers between devices: 242 us -> 0 us
  local copies, waits for them, and re-layouts: 39.6 us -> 72.8 us
  starting transfers between devices: 25.1 us -> 0 us
  between operations: 20.6 us -> 2.49 us
  other arithmetic: 13.9 us -> 0.01 us
    unnamed x1 -> x0, blocking collectives: 340 us -> none
    pallas_call x0 -> x3, Pallas kernels: none -> 318 us  [the longest x1 203 us: shard_body(): pl.pallas_call(reduce_kernel, out_shape=(jax.ShapeDtypeStruct((40, 8, 102...]
    all_gather x4 -> x0, waiting for transfers between devices: 239 us -> none  [shard_body(): lax.all_gather(layer_state[0], 'data', axis=0, tiled=True)]
    unnamed x0 -> x2, matrix products: none -> 59.9 us
    dot_general x4 -> x2, matrix products: 109 us -> 51.8 us  [mat_tn(): lax.dot_general(left, right, (((0,), (0,)), ((), ())), preferred_element_...]
    psum x1 -> x0, blocking collectives: 42.7 us -> none  [shard_body(): grad_norm = jnp.sqrt(lax.psum(local_sq, 'data'))]
    unnamed x4 -> x0, starting transfers between devices: 24.8 us -> none
    pad x0 -> x2, local copies, waits for them, and re-layouts: none -> 20.5 us  [shard_body(): local[k] = jnp.pad(local[k], ((0, 0), (0, 64))).reshape(DEVS, DOWN, 1024)]
  transfers between devices with their start and end apart: 10 -> 0, of which waited for: 5 -> 0; matrix products, arithmetic and copies ran while one was open for 49% -> 0% of each run, Pallas kernels for 0% -> 0%
where the time goes in v1:
time: 708 us; the launch traced here: 699 us
  Pallas kernels  318 us (45%)
  matrix products  305 us (43%)
  local copies, waits for them, and re-layouts  72.8 us (10%)
    pallas_call x1, Pallas kernels, shard_body(): pl.pallas_call(reduce_kernel, out_shape=(jax.ShapeDtypeStruct((40, 8, 102...  203 us
    dot_general x3, matrix products, mat_nt(): lax.dot_general(left, right, (((1,), (1,)), ((), ())), preferred_element_...  110 us
    pallas_call x1, Pallas kernels, shard_body(): pl.pallas_call(gather_kernel, out_shape=(jax.ShapeDtypeStruct((10, 32, 32...  95.3 us
    unnamed x2, matrix products  59.9 us
    dot_general x2, matrix products, mat_tn(): lax.dot_general(left, right, (((0,), (0,)), ((), ())), preferred_element_...  51.8 us
    dot_general x1, matrix products, fwd_bwd(): pre_up1 = jnp.dot(rows_in, w_up1, preferred_element_type=jnp.float32)  34 us
    unnamed x52, local copies, waits for them, and re-layouts  32.5 us
    dot_general x1, matrix products, fwd_bwd(): pre_up2 = jnp.dot(mid_act, w_up2, preferred_element_type=jnp.float32)  26.6 us

profile of v1, /device:TPU:0, one launch (start us, length us, event | category | flops | bytes accessed | tf_op | source)
XLA Modules:
  0.0 699.1 jit_solution(367913211734631426)
XLA Ops:
  0.7 34.0 %multiply_convert_fusion.1 = (bf16[4096,2560]{1,0:T(8,128)(2,1)}, f32[4096,2560]{1,0:T(8,128)}) fusion(bf16[4096,960]{0,1:T(8,128)(2,1)} %param.20, bf16[960,2560]{1,0:T(8,128)(2,1)} %param.22), kind=kOutput, calls=%fused_computation.16 | convolution fusion | flops 20185088000 | bytes 75694080 | tf_op jit(solution)/shard_map/dot_general | solution.py:45
  34.7 23.6 %convolution_convert_fusion.3 = bf16[4096,960]{0,1:T(8,128)(2,1)S(1)} fusion(bf16[4096,2560]{1,0:T(8,128)(2,1)} %get-tuple-element.74, bf16[2560,960]{0,1:T(8,128)(2,1)S(1)} %copy-done.16), kind=kOutput, calls=%fused_computation.22 | convolution fusion | flops 20136591360 | bytes 33751040 | tf_op jit(solution)/shard_map/dot_general | solution.py:48
  58.3 3.0 copy-done.18
  61.4 26.6 %fusion.16 = f32[4096,2560]{1,0:T(8,128)} fusion(bf16[4096,960]{0,1:T(8,128)(2,1)S(1)} %convolution_convert_fusion.3, bf16[960,2560]{1,0:T(8,128)(2,1)S(1)} %bitcast.52), kind=kOutput, calls=%fused_computation.29 | convolution fusion | flops 20132659200 | bytes 54722560 | tf_op jit(solution)/shard_map/dot_general | solution.py:49
  87.9 31.0 %fusion.12 = f32[2560,960]{1,0:T(8,128)} fusion(bf16[4096,960]{0,1:T(8,128)(2,1)} %param.21, f32[4096,2560]{1,0:T(8,128)} %fusion.16), kind=kOutput, calls=%fused_computation.20 | convolution fusion | flops 20185088000 | bytes 59637760
  118.9 10.2 %pad.7.clone = f32[2560,1024]{1,0:T(8,128)} pad(f32[2560,960]{1,0:T(8,128)} %fusion.12, f32[]{:T(128)} %constant.4.clone.1), padding=0_0x0_64 | pad | bytes 20316164 | tf_op jit(solution)/shard_map/jit(_pad)/pad | solution.py:309
  129.1 42.1 %fusion.5 = bf16[4096,2560]{1,0:T(8,128)(2,1)} fusion(f32[4096,2560]{1,0:T(8,128)} %fusion.16, bf16[4096,960]{0,1:T(8,128)(2,1)S(1)} %copy-done.14, bf16[2560,960]{0,1:T(8,128)(2,1)S(1)} %copy-done.15), kind=kOutput, calls=%fused_computation.7 | convolution fusion | flops 20258488320 | bytes 75694080 | tf_op jit(solution)/shard_map/dot_general | solution.py:31
  171.3 27.1 %fusion.17.g3 = f32[960,2560]{1,0:T(8,128)} fusion(bf16[4096,960]{0,1:T(8,128)(2,1)} %copy-done.18, bf16[4096,2560]{1,0:T(8,128)(2,1)} %fusion.5), kind=kOutput, calls=%fused_computation.30 | convolution fusion | flops 20132659200 | bytes 38666240 | tf_op jit(solution)/shard_map/dot_general | solution.py:35
  198.4 25.7 %convolution_convert_fusion.2 = bf16[4096,960]{0,1:T(8,128)(2,1)} fusion(bf16[4096,2560]{1,0:T(8,128)(2,1)S(1)} %copy-done.17, bf16[960,2560]{1,0:T(8,128)(2,1)} %param.24), kind=kOutput, calls=%fused_computation.21 | convolution fusion | flops 20136591360 | bytes 33751040 | tf_op jit(solution)/shard_map/dot_general | solution.py:31
  224.1 29.0 %fusion.18 = f32[2560,960]{1,0:T(8,128)} fusion(bf16[4096,960]{0,1:T(8,128)(2,1)} %convolution_convert_fusion.2, bf16[4096,2560]{1,0:T(8,128)(2,1)} %get-tuple-element.74), kind=kOutput, calls=%fused_computation.31 | convolution fusion | flops 20132659200 | bytes 38666240
  253.1 10.3 %pad.8.clone = f32[2560,1024]{1,0:T(8,128)} pad(f32[2560,960]{1,0:T(8,128)} %fusion.18, f32[]{:T(128)} %constant.4.clone.1), padding=0_0x0_64 | pad | bytes 20316164 | tf_op jit(solution)/shard_map/jit(_pad)/pad | solution.py:309
  263.4 41.8 %fusion.11.clone.4 = bf16[4096,2560]{1,0:T(8,128)(2,1)} fusion(f32[4096,2560]{1,0:T(8,128)} %get-tuple-element.75, bf16[4096,960]{0,1:T(8,128)(2,1)} %convolution_convert_fusion.2, bf16[2560,960]{0,1:T(8,128)(2,1)S(1)} %bitcast.54), kind=kOutput, calls=%fused_computation.13.clone.clone.clone.1 | convolution fusion | flops 20258488320 | bytes 75694080 | tf_op jit(solution)/shard_map/dot_general | solution.py:31
  305.1 24.6 %convolution_bitcast_fusion.g1 = f32[960,2560]{1,0:T(8,128)} fusion(bf16[4096,960]{0,1:T(8,128)(2,1)S(1)} %bitcast.50, bf16[4096,2560]{1,0:T(8,128)(2,1)} %fusion.11.clone.4), kind=kOutput, calls=%fused_computation.23 | convolution fusion | flops 20132659200 | bytes 38666240 | tf_op jit(solution)/shard_map/dot_general | solution.py:35
  329.8 203.3 %reduce.1 = (f32[40,8,1024]{2,1,0:T(8,128)}, f32[8,128]{1,0:T(8,128)}) custom-call(f32[32,80,1024]{2,1,0:T(8,128)} %bitcast.45, f32[960,2560]{1,0:T(8,128)} %fusion.17.g3, f32[32,80,1024]{2,1,0:T(8,128)} %bitcast.46, f32[960,2560]{1,0:T(8,128)} %convolution_bitcast_fusion.g1), custom_call_target="tpu_custom_call" | custom-call | tf_op jit(solution)/shard_map/reduce/pallas_call | solution.py:310
  534.4 1.3 copy-done
  535.7 1.0 copy-done.1
  536.7 1.0 copy-done.2
  537.6 1.0 copy-done.3
  538.6 1.0 copy-done.4
  539.6 1.0 copy-done.5
  540.5 1.0 copy-done.6
  541.5 1.0 copy-done.7
  542.5 1.0 copy-done.8
  545.4 1.0 copy-done.11
  546.4 1.0 copy-done.12
  548.0 95.3 %gather.1 = (bf16[10,32,32,512]{3,2,1,0:T(8,128)(2,1)}, bf16[10,32,16,1024]{3,2,1,0:T(8,128)(2,1)}) custom-call(f32[40,8,1024]{2,1,0:T(8,128)S(1)} %copy-done, f32[8,128]{1,0:T(8,128)S(1)} %copy-done.13, f32[1]{0:T(128)} %bitcast.41.lr, f32[1]{0:T(128)} %bitcast.43.clip, f32[80,960]{1,0:T(8,128)S(1)} %copy-done.1, f32[80,960]{1,0:T(8,128)S(1)} %copy-done.2, ...), custom_call_target="tpu_custom_call" | custom-call | tf_op jit(solution)/shard_map/gather/pallas_call | solution.py:323
  643.4 19.8 %finish.1 = (bf16[2,960,2560]{2,1,0:T(8,128)(2,1)}, bf16[2,32,80,960]{3,2,1,0:T(8,128)(2,1)}, f32[80,960]{1,0:T(8,128)}, f32[80,960]{1,0:T(8,128)}, f32[80,960]{...) custom-call(bf16[10,32,32,512]{3,2,1,0:T(8,128)(2,1)} %get-tuple-ele, ...), custom_call_target="tpu_custom_call" | custom-call | tf_op jit(solution)/shard_map/finish/pallas_call | solution.py:335
  663.1 8.4 %slice_bitcast_fusion = (bf16[960,2560]{1,0:T(8,128)(2,1)}, bf16[960,2560]{1,0:T(8,128)(2,1)}) fusion(bf16[2,960,2560]{2,1,0:T(8,128)(2,1)} %get-tuple-element.39), kind=kLoop, calls=%fused_computation.24 | loop fusion | bytes 19660800 | tf_op jit(solution)/shard_map/squeeze | solution.py:349
  671.5 10.2 %fusion.15 = (bf16[1,32,80,960]{3,2,1,0:T(8,128)(2,1)}, bf16[1,32,80,960]{3,2,1,0:T(8,128)(2,1)}) fusion(bf16[2,32,80,960]{3,2,1,0:T(8,128)(2,1)} %get-tuple-element.40), kind=kLoop, calls=%fused_computation.28 | loop fusion | bytes 19660800 | tf_op jit(solution)/shard_map/slice | solution.py:349
  681.7 7.9 %copy.39 = bf16[2560,960]{0,1:T(8,128)(2,1)} copy(bf16[2560,960]{1,0:T(8,128)(2,1)} %bitcast.48) | data formatting | bytes 9830400
  689.6 7.9 %copy.40 = bf16[2560,960]{0,1:T(8,128)(2,1)} copy(bf16[2560,960]{1,0:T(8,128)(2,1)} %bitcast.47) | data formatting | bytes 9830400
  697.5 1.2 slice.21
  (41 shorter events, 2.7 us)
Async XLA Ops:
  0.7 34.0 %copy-start.16 = (bf16[2560,960]{0,1:T(8,128)(2,1)S(1)}, bf16[2560,960]{0,1:T(8,128)(2,1)}, u32[]{:S(2)}) copy-start(bf16[2560,960]{0,1:T(8,128)(2,1)} %param.23) | copy-start | bytes 14745604
  0.7 60.7 %slice-start.2 = ((s8[4915200]{0:T(1024)(128)(4,1)}), s8[4194304]{0:T(1024)(128)(4,1)S(1)}, s32[]{:S(2)}) async-start(s8[4915200]{0:T(1024)(128)(4,1)} %bitcast.51), calls=%async_computation.2 | async-start | bytes 8388608
  34.7 26.7 %slice-start.3 = ((s8[4915200]{0:T(1024)(128)(4,1)}), s8[720896]{0:T(1024)(128)(4,1)S(1)}, s32[]{:S(2)}) async-start(s8[4915200]{0:T(1024)(128)(4,1)} %bitcast.51), calls=%async_computation.3 | async-start | bytes 1441792
  58.3 3.0 copy-start.18
  118.9 10.2 %copy-start.14 = (bf16[4096,960]{0,1:T(8,128)(2,1)S(1)}, bf16[4096,960]{0,1:T(8,128)(2,1)}, u32[]{:S(2)}) copy-start(bf16[4096,960]{0,1:T(8,128)(2,1)} %param.21) | copy-start | bytes 23592964
  118.9 10.2 %copy-start.15 = (bf16[2560,960]{0,1:T(8,128)(2,1)S(1)}, bf16[2560,960]{0,1:T(8,128)(2,1)}, u32[]{:S(2)}) copy-start(bf16[2560,960]{0,1:T(8,128)(2,1)} %param.25) | copy-start | bytes 14745604
  171.3 27.1 %copy-start.17 = (bf16[4096,2560]{1,0:T(8,128)(2,1)S(1)}, bf16[4096,2560]{1,0:T(8,128)(2,1)}, u32[]{:S(2)}) copy-start(bf16[4096,2560]{1,0:T(8,128)(2,1)} %fusion.5) | copy-start | bytes 62914564
  198.4 64.9 %slice-start.4 = ((s8[4915200]{0:T(1024)(128)(4,1)}), s8[4194304]{0:T(1024)(128)(4,1)S(1)}, s32[]{:S(2)}) async-start(s8[4915200]{0:T(1024)(128)(4,1)} %bitcast.53), calls=%async_computation.4 | async-start | bytes 8388608
  224.1 39.2 %slice-start.5 = ((s8[4915200]{0:T(1024)(128)(4,1)}), s8[720896]{0:T(1024)(128)(4,1)S(1)}, s32[]{:S(2)}) async-start(s8[4915200]{0:T(1024)(128)(4,1)} %bitcast.53), calls=%async_computation.5 | async-start | bytes 1441792
  253.1 52.0 %slice-start = ((s8[7864320]{0:T(1024)(128)(4,1)}), s8[3670016]{0:T(1024)(128)(4,1)S(1)}, s32[]{:S(2)}) async-start(s8[7864320]{0:T(1024)(128)(4,1)} %bitcast.49), calls=%async_computation | async-start | bytes 7340032
  263.4 41.8 %slice-start.1 = ((s8[7864320]{0:T(1024)(128)(4,1)}), s8[4194304]{0:T(1024)(128)(4,1)S(1)}, s32[]{:S(2)}) async-start(s8[7864320]{0:T(1024)(128)(4,1)} %bitcast.49), calls=%async_computation.1 | async-start | bytes 8388608
  534.4 1.3 copy-start
  535.7 1.0 copy-start.1
  536.7 1.0 copy-start.2
  537.6 1.0 copy-start.3
  538.6 1.0 copy-start.4
  539.6 1.0 copy-start.5
  540.5 1.0 copy-start.6
  541.5 1.0 copy-start.7
  542.5 1.0 copy-start.8
  543.5 1.0 copy-start.9
  544.4 1.0 copy-start.10
  545.4 1.0 copy-start.11
  546.4 1.0 copy-start.12
  547.4 0.7 copy-start.13
